TPU v7x, 32 devices: a whole 2x2x4 slice. The times are simulated.
32 devices in a mesh: shard: 8 (over y, x, core), replica: 4 (over z).
Axes of the slice: x: 2, y: 2, z: 4, core: 2. Of those that a mesh axis runs over, the one named last changes fastest.
Arguments:
- custkey: int32 [262144], P(('shard', 'replica')), may hold values from 0 to 8191
- quarter: int32 [262144], P(('shard', 'replica')), may hold values from 0 to 27
- revenue: float32 [262144], P(('shard', 'replica')), may hold values from -6 to 6
- segment: int32 [8192], P('shard'), may hold values from 0 to 4
- rate: bfloat16 [8192], P('shard'), may hold values from 0.25 to 4
Outputs:
- cube: float32 [5, 28], replicated
All inputs are finite; a program needn't handle non-finite values.
Results may differ from a plain program's by a relative error of at most 0.0003.
Values may be sent and summed in bfloat16 or wider, within the bound.
No kernel may reach another device: no remote copies, remote signals or barrier semaphores. Data moves between devices by JAX's collectives and lax.ppermute only.
A program may use at most 64 MiB of HBM per device.

v0:
```python
import math

import jax
import jax.numpy as jnp
from jax import lax
from jax.sharding import PartitionSpec as P

SEGMENTS = 5
QUARTERS = 28


def cube_rows(cell, weight):
    length = cell.shape[0]
    step_size = math.gcd(length, 2048)
    cell_ids = jnp.arange(SEGMENTS * QUARTERS, dtype=jnp.int32)

    def inner(index, total):
        cells = lax.dynamic_slice_in_dim(cell, index * step_size, step_size)
        weights = lax.dynamic_slice_in_dim(weight, index * step_size, step_size)
        onehot = (cells[:, None] == cell_ids[None, :]).astype(jnp.float32)
        return total + jnp.dot(
            weights[None, :],
            onehot,
            preferred_element_type=jnp.float32,
            precision=lax.Precision.HIGHEST,
        )

    empty = jnp.zeros((1, SEGMENTS * QUARTERS), jnp.float32)
    return lax.fori_loop(0, length // step_size, inner, empty)


def per_device(custkey, quarter, revenue, segment, rate):
    keys, quarters, revenues = (custkey, quarter, revenue)
    usable = jnp.ones(keys.shape, jnp.bool_)
    table = (segment.astype(jnp.bfloat16), rate)
    pieces = (
        lax.all_gather(table[0], "shard", axis=0, tiled=True),
        lax.all_gather(table[1], "shard", axis=0, tiled=True),
    )
    rows = pieces[0].shape[0]
    inside = usable & (keys >= 0) & (keys < rows)
    safe = jnp.clip(keys, 0, rows - 1)
    seg_piece = jnp.take(pieces[0], safe).astype(jnp.float32)
    factor_piece = jnp.take(pieces[1], safe).astype(jnp.float32)
    seg_found = jnp.where(inside, seg_piece, 0.0)
    factor = jnp.where(inside, factor_piece, 0.0)
    weight = revenues * factor
    cell = seg_found.astype(jnp.int32) * QUARTERS + quarters
    partial_flat = cube_rows(cell, weight)
    partial_cube = partial_flat.reshape(SEGMENTS, QUARTERS)
    grouped = lax.psum(partial_cube, "replica")
    return lax.psum(grouped, "shard")


def solution(mesh):
    return jax.shard_map(
        per_device,
        mesh=mesh,
        in_specs=(
            P(("shard", "replica")),
            P(("shard", "replica")),
            P(("shard", "replica")),
            P("shard"),
            P("shard"),
        ),
        out_specs=P(),
        check_vma=False,
    )
```

profile of v0, /device:TPU:0, one launch (start us, length us, event | category | flops | bytes accessed | tf_op | source)
XLA Modules:
  0.0 151.1 jit_solution(11290103970034484259)
XLA Ops:
  0.0 0.0 copy-start
  0.0 0.7 convert_element_type.16
  0.7 10.4 %all_gather.7 = bf16[8192]{0:T(1024)(128)(2,1)S(1)} all-gather(bf16[1024]{0:T(1024)(128)(2,1)S(1)} %convert_element_type.16), channel_id=1, replica_groups=mesh['shard'=8,'replica'=4] {'shard'}, dimensions={0}, use_global_device_ids=true | all-gather | bytes 18432 | tf_op jit(solution)/shard_map/all_gather | solution.py:37
  11.1 8.9 %all_gather.6 = bf16[8192]{0:T(1024)(128)(2,1)S(1)} all-gather(bf16[1024]{0:T(1024)(128)(2,1)} %param.13), channel_id=1, replica_groups=mesh['shard'=8,'replica'=4] {'shard'}, dimensions={0}, use_global_device_ids=true | all-gather | bytes 18432 | tf_op jit(solution)/shard_map/all_gather | solution.py:38
  20.0 0.0 copy-done
  20.0 50.7 %gather_fusion.1 = bf16[8192]{0:T(1024)(128)(2,1)S(1)} fusion(bf16[8192]{0:T(1024)(128)(2,1)S(1)} %all_gather.7, s32[8192]{0:T(1024)S(1)} %fusion.5), kind=kCustom, calls=%fused_computation.1.clone | custom fusion | bytes 65536 | tf_op jit(solution)/shard_map/jit(_take)/gather | solution.py:43
  70.7 0.0 copy-start.2
  70.7 50.7 %gather_fusion = bf16[8192]{0:T(1024)(128)(2,1)S(1)} fusion(bf16[8192]{0:T(1024)(128)(2,1)S(1)} %all_gather.6, s32[8192]{0:T(1024)S(1)} %fusion.5), kind=kCustom, calls=%fused_computation.clone | custom fusion | bytes 65536 | tf_op jit(solution)/shard_map/jit(_take)/gather | solution.py:44
  121.5 0.0 copy-done.2
  121.5 0.0 copy-start.1
  121.5 0.7 copy-done.1
  122.3 3.3 %while.14 = (s32[]{:T(128)}, f32[1,140]{1,0:T(1,128)S(1)}, f32[8192]{0:T(1024)S(1)}, s32[8192]{0:T(1024)S(1)}, s32[]{:T(128)}, /*index=5*/s32[]{:T(128)}, s32[]{:T(128)}, s32[]{:T(128)}) while((s32[]{:T(128)}, f32[1,140]{1,0:T(1,128)S(1)}, f32[8192]{0:T(1024)S(1)}, s32[8192]{0:T(1024)S(1)}, s32[]{:T(128)}, /*index=5*/s32[]{:T(128)}, ...), condition=%wide.region_1.3_spmd.clone, body=%wide.region_0.2_spmd.clone.sunk | while | flops 3727647 | bytes 50429 | solution.py:29
  122.3 0.8 fusion.10
  123.1 0.8 fusion.10
  123.9 0.8 fusion.10
  124.7 0.8 fusion.10
  125.5 0.5 broadcast.21
  126.1 0.7 reduce.3
  126.7 0.1 reshape.15
  126.8 11.9 %psum.14 = f32[5,28]{1,0:T(8,128)S(1)} all-reduce(f32[5,28]{1,0:T(8,128)S(1)} %reshape.15), channel_id=1, replica_groups=mesh['shard'=8,'replica'=4] {'replica'}, use_global_device_ids=true, to_apply=%region_2.4 | all-reduce | flops 140 | bytes 1120 | tf_op jit(solution)/shard_map/psum | solution.py:51
  138.7 12.4 %psum.15 = f32[5,28]{1,0:T(8,128)} all-reduce(f32[5,28]{1,0:T(8,128)S(1)} %psum.14), channel_id=1, replica_groups=mesh['shard'=8,'replica'=4] {'shard'}, use_global_device_ids=true, to_apply=%region_3.5 | all-reduce | flops 140 | bytes 1120 | tf_op jit(solution)/shard_map/psum | solution.py:52
  (12 shorter events, 0.1 us)
Async XLA Ops:
  0.0 20.0 %copy-start = (s32[8192]{0:T(1024)S(1)}, s32[8192]{0:T(1024)}, u32[]{:S(2)}) copy-start(s32[8192]{0:T(1024)} %param.9) | copy-start | bytes 98308
  70.7 50.7 %copy-start.2 = (s32[8192]{0:T(1024)S(1)}, s32[8192]{0:T(1024)}, u32[]{:S(2)}) copy-start(s32[8192]{0:T(1024)} %param.10) | copy-start | bytes 98308
  121.5 0.8 copy-start.1
where the time goes:
time: 151 us
  local copies, waits for them, and re-layouts  103 us (68%)
  blocking collectives  43.6 us (29%)
  matrix products  3.21 us (2%)
    gather x1, local copies, waits for them, and re-layouts, per_device(): seg_piece = jnp.take(pieces[0], safe).astype(jnp.float32)  50.7 us
    gather x1, local copies, waits for them, and re-layouts, per_device(): factor_piece = jnp.take(pieces[1], safe).astype(jnp.float32)  50.7 us
    psum x1, blocking collectives, per_device(): return lax.psum(grouped, 'shard')  12.4 us
    psum x1, blocking collectives, per_device(): grouped = lax.psum(partial_cube, 'replica')  11.9 us
    all_gather x1, blocking collectives, per_device(): lax.all_gather(table[0], 'shard', axis=0, tiled=True)  10.4 us
    all_gather x1, blocking collectives, per_device(): lax.all_gather(table[1], 'shard', axis=0, tiled=True)  8.88 us
    dot_general x4, matrix products, inner(): jnp.dot(weights[None, :], onehot, preferred_element_type=jnp.float32, pre...  3.21 us

commit v1 on v0

v1 whole, which is shorter than its diff:
```python
import jax
import jax.numpy as jnp
from jax import lax
from jax.experimental import pallas as pl
from jax.experimental.pallas import tpu as pltpu
from jax.sharding import PartitionSpec as P

SEGMENTS = 5
QUARTERS = 28
SUBLANES = 8
LANES = 128
STEP = 8.0


def sublane_sums(parts):
    row = lax.broadcasted_iota(jnp.int32, (SUBLANES, LANES), 0)

    def merge(a, b, width, bit):
        keep = (row & bit) == 0
        if b is None:
            return a + pltpu.roll(a, width, 0)
        return jnp.where(keep, a, b) + pltpu.roll(jnp.where(keep, b, a), width, 0)

    a0, a1, a2, a3, a4 = parts
    a0 = merge(a0, a4, 4, 4)
    a1, a2, a3 = (merge(a, None, 4, 4) for a in (a1, a2, a3))
    def fold(a, b, width):
        keep = (row & width) == 0
        up = jnp.where(keep, pltpu.roll(a, SUBLANES - width, 0), pltpu.roll(b, width, 0))
        return jnp.where(keep, a, b) + up

    a0, a1 = fold(a0, a2, 2), fold(a1, a3, 2)
    return fold(a0, a1, 1)


def cube_kernel(table_ref, custkey_ref, quarter_ref, revenue_ref, out_ref):
    rows = table_ref.shape[0]
    chunks = custkey_ref.shape[0] // SUBLANES
    at = [pl.ds(c * SUBLANES, SUBLANES) for c in range(chunks)]
    keys = [custkey_ref[a, :] for a in at]
    high = [k // LANES for k in keys]
    low = [k % LANES for k in keys]

    def look(step, found):
        base = pl.multiple_of(step * SUBLANES, SUBLANES)
        found = list(found)
        for r in range(SUBLANES):
            line = jnp.broadcast_to(table_ref[pl.ds(base + r, 1), :], (SUBLANES, LANES))
            for c in range(chunks):
                got = jnp.take_along_axis(line, low[c], axis=1)
                found[c] = jnp.where(high[c] == base + r, got, found[c])
        return tuple(found)

    zero = jnp.zeros((SUBLANES, LANES), jnp.float32)
    found = lax.fori_loop(0, rows // SUBLANES, look, (zero,) * chunks)
    weights = []
    for c in range(chunks):
        segment = jnp.floor(found[c] * (1.0 / STEP))
        weight = revenue_ref[at[c], :] * (found[c] - segment * STEP)
        weights.append([jnp.where(segment == s, weight, 0.0) for s in range(SEGMENTS)])
    quarters = [quarter_ref[a, :] for a in at]
    lane = lax.broadcasted_iota(jnp.int32, (SUBLANES, LANES), 1)
    cube = zero
    for q in range(QUARTERS):
        inside = [x == q for x in quarters]
        parts = []
        for s in range(SEGMENTS):
            total = zero
            for c in range(chunks):
                total = total + jnp.where(inside[c], weights[c][s], 0.0)
            parts.append(total)
        sums = jnp.sum(sublane_sums(parts), axis=1, keepdims=True)
        cube = jnp.where(lane == q, sums, cube)
    for d in range(out_ref.shape[0]):
        out_ref[d] = cube


def solution(mesh):
    shards = mesh.shape["shard"]
    everyone = shards * mesh.shape["replica"]

    def per_device(custkey, quarter, revenue, segment, rate):
        mine = segment.astype(jnp.float32) * STEP + rate.astype(jnp.float32)
        mine = mine.reshape(-1, LANES)
        table = lax.all_to_all(
            jnp.broadcast_to(mine[None], (shards, *mine.shape)), "shard", 0, 0
        )
        partial_cubes = pl.pallas_call(
            cube_kernel,
            out_shape=jax.ShapeDtypeStruct((everyone, SUBLANES, LANES), jnp.float32),
        )(
            table.reshape(-1, LANES),
            custkey.reshape(-1, LANES),
            quarter.reshape(-1, LANES),
            revenue.reshape(-1, LANES),
        )
        cubes = lax.all_to_all(partial_cubes, ("shard", "replica"), 0, 0)
        return jnp.sum(cubes, axis=0)[:SEGMENTS, :QUARTERS]

    return jax.shard_map(
        per_device,
        mesh=mesh,
        in_specs=(
            P(("shard", "replica")),
            P(("shard", "replica")),
            P(("shard", "replica")),
            P("shard"),
            P("shard"),
        ),
        out_specs=P(),
        check_vma=False,
    )
```

time: 151 us -> 27.8 us (0.18)
  local copies, waits for them, and re-layouts: 103 us -> 0.01 us
  blocking collectives: 43.6 us -> 22.3 us
  Pallas kernels: 0 us -> 3.92 us
  matrix products: 3.21 us -> 0 us
    gather x2 -> x0, local copies, waits for them, and re-layouts: 101 us -> none  [the longest x1 50.7 us: per_device(): seg_piece = jnp.take(pieces[0], safe).astype(jnp.float32)]
    psum x2 -> x0, blocking collectives: 24.3 us -> none  [the longest x1 12.4 us: per_device(): return lax.psum(grouped, 'shard')]
    all_to_all x0 -> x2, blocking collectives: none -> 22.3 us  [the longest x1 12.4 us: per_device(): cubes = lax.all_to_all(partial_cubes, ('shard', 'replica'), 0, 0)]
    all_gather x2 -> x0, blocking collectives: 19.3 us -> none  [the longest x1 10.4 us: per_device(): lax.all_gather(table[0], 'shard', axis=0, tiled=True)]
    pallas_call x0 -> x1, Pallas kernels: none -> 3.92 us  [per_device(): pl.pallas_call(cube_kernel, out_shape=jax.ShapeDtypeStruct((everyone, SUB...]
    dot_general x4 -> x0, matrix products: 3.21 us -> none  [inner(): jnp.dot(weights[None, :], onehot, preferred_element_type=jnp.float32, pre...]
where the time goes in v1:
time: 27.8 us; the launch traced here: 27.6 us
  blocking collectives  22.3 us (80%)
  Pallas kernels  3.92 us (14%)
  other arithmetic  1.33 us (5%)
    all_to_all x1, blocking collectives, per_device(): cubes = lax.all_to_all(partial_cubes, ('shard', 'replica'), 0, 0)  12.4 us
    all_to_all x1, blocking collectives, per_device(): lax.all_to_all(jnp.broadcast_to(mine[None], (shards, *mine.shape)), 'shar...  9.93 us
    pallas_call x1, Pallas kernels, per_device(): pl.pallas_call(cube_kernel, out_shape=jax.ShapeDtypeStruct((everyone, SUB...  3.92 us
    broadcast_in_dim x1, other arithmetic, per_device(): jnp.broadcast_to(mine[None], (shards, *mine.shape))  0.71 us
    reduce_sum x1, other arithmetic, per_device(): return jnp.sum(cubes, axis=0)[:SEGMENTS, :QUARTERS]  0.63 us

profile of v1, /device:TPU:0, one launch (start us, length us, event | category | flops | bytes accessed | tf_op | source)
XLA Modules:
  0.0 27.6 jit_solution(9664816963819837815)
XLA Ops:
  0.0 0.7 %add_bitcast_fusion = f32[8,128]{1,0:T(8,128)S(1)} fusion(bf16[1024]{0:T(1024)(128)(2,1)} %param.9, s32[1024]{0:T(1024)} %param.8), kind=kLoop, calls=%fused_computation | loop fusion | flops 4096 | bytes 10240 | tf_op jit(solution)/shard_map/broadcast_in_dim | solution.py:86
  0.7 9.9 %all_to_all.10 = f32[8,8,128]{2,1,0:T(8,128)} all-to-all(f32[8,8,128]{2,1,0:T(8,128)S(1)} %broadcast_in_dim.8), channel_id=1, replica_groups=mesh['shard'=8,'replica'=4] {'shard'}, dimensions={0} | all-to-all | bytes 65536 | tf_op jit(solution)/shard_map/all_to_all | solution.py:85
  10.6 3.9 %shard_map.55 = f32[32,8,128]{2,1,0:T(8,128)} custom-call(f32[64,128]{1,0:T(8,128)} %bitcast.7, s32[64,128]{1,0:T(8,128)} %bitcast.8, s32[64,128]{1,0:T(8,128)} %bitcast.9, f32[64,128]{1,0:T(8,128)} %bitcast.10), custom_call_target="tpu_custom_call" | custom-call | tf_op jit(solution)/shard_map/pallas_call | solution.py:88
  14.6 12.4 %all_to_all.11 = f32[32,8,128]{2,1,0:T(8,128)S(1)} all-to-all(f32[32,8,128]{2,1,0:T(8,128)} %shard_map.55), channel_id=1, replica_groups=mesh['shard'=8,'replica'=4] {'shard','replica'}, dimensions={0} | all-to-all | bytes 262144 | tf_op jit(solution)/shard_map/all_to_all | solution.py:97
  26.9 0.6 %reduce_sum.9 = f32[8,128]{1,0:T(8,128)} reduce(f32[32,8,128]{2,1,0:T(8,128)S(1)} %all_to_all.11, f32[]{:T(128)} %constant.1.clone.1), dimensions={0}, to_apply=%region_0.0 | reduce | flops 31744 | bytes 135172 | tf_op jit(solution)/shard_map/reduce_sum | solution.py:98
  (1 shorter events, 0.0 us)

commit v2 on v1

--- a/solution.py
+++ b/solution.py
@@ -88,6 +88,7 @@
         partial_cubes = pl.pallas_call(
             cube_kernel,
             out_shape=jax.ShapeDtypeStruct((everyone, SUBLANES, LANES), jnp.float32),
+            compiler_params=pltpu.CompilerParams(vmem_limit_bytes=4 * 2**20),
         )(
             table.reshape(-1, LANES),
             custkey.reshape(-1, LANES),

time: 27.8 us -> 26.2 us (0.942)
  Pallas kernels: 3.92 us -> 2.48 us
    pallas_call x1, Pallas kernels: 3.92 us -> 2.48 us  [per_device(): pl.pallas_call(cube_kernel, out_shape=jax.ShapeDtypeStruct((everyone, SUB...]
where the time goes in v2:
time: 26.2 us; the launch traced here: 26 us
  blocking collectives  22.1 us (84%)
  Pallas kernels  2.48 us (9%)
  other arithmetic  1.33 us (5%)
    all_to_all x1, blocking collectives, per_device(): cubes = lax.all_to_all(partial_cubes, ('shard', 'replica'), 0, 0)  12.2 us
    all_to_all x1, blocking collectives, per_device(): lax.all_to_all(jnp.broadcast_to(mine[None], (shards, *mine.shape)), 'shar...  9.97 us
    pallas_call x1, Pallas kernels, per_device(): pl.pallas_call(cube_kernel, out_shape=jax.ShapeDtypeStruct((everyone, SUB...  2.48 us
    broadcast_in_dim x1, other arithmetic, per_device(): jnp.broadcast_to(mine[None], (shards, *mine.shape))  0.71 us
    reduce_sum x1, other arithmetic, per_device(): return jnp.sum(cubes, axis=0)[:SEGMENTS, :QUARTERS]  0.63 us

profile of v2, /device:TPU:0, one launch (start us, length us, event | category | flops | bytes accessed | tf_op | source)
XLA Modules:
  0.0 26.0 jit_solution(10311816802012987246)
XLA Ops:
  0.0 0.7 %add_bitcast_fusion = f32[8,128]{1,0:T(8,128)S(1)} fusion(bf16[1024]{0:T(1024)(128)(2,1)} %param.9, s32[1024]{0:T(1024)} %param.8), kind=kLoop, calls=%fused_computation | loop fusion | flops 4096 | bytes 10240 | tf_op jit(solution)/shard_map/broadcast_in_dim | solution.py:86
  0.7 0.0 copy-start.2
  0.7 0.0 copy-start
  0.7 0.0 copy-start.1
  0.7 10.0 %all_to_all.10 = f32[8,8,128]{2,1,0:T(8,128)S(1)} all-to-all(f32[8,8,128]{2,1,0:T(8,128)S(1)} %broadcast_in_dim.8), channel_id=1, replica_groups=mesh['shard'=8,'replica'=4] {'shard'}, dimensions={0} | all-to-all | bytes 65536 | tf_op jit(solution)/shard_map/all_to_all | solution.py:85
  10.7 0.0 copy-done.2
  10.7 0.0 copy-done
  10.7 0.0 copy-done.1
  10.7 2.5 %shard_map.55 = f32[32,8,128]{2,1,0:T(8,128)S(1)} custom-call(f32[64,128]{1,0:T(8,128)S(1)} %bitcast.7, s32[64,128]{1,0:T(8,128)S(1)} %bitcast.8, s32[64,128]{1,0:T(8,128)S(1)} %bitcast.9, f32[64,128]{1,0:T(8,128)S(1)} %bitcast.10), custom_call_target="tpu_custom_call" | custom-call | tf_op jit(solution)/shard_map/pallas_call | solution.py:88
  13.2 12.2 %all_to_all.11 = f32[32,8,128]{2,1,0:T(8,128)S(1)} all-to-all(f32[32,8,128]{2,1,0:T(8,128)S(1)} %shard_map.55), channel_id=1, replica_groups=mesh['shard'=8,'replica'=4] {'shard','replica'}, dimensions={0} | all-to-all | bytes 262144 | tf_op jit(solution)/shard_map/all_to_all | solution.py:98
  25.4 0.6 %reduce_sum.9 = f32[8,128]{1,0:T(8,128)} reduce(f32[32,8,128]{2,1,0:T(8,128)S(1)} %all_to_all.11, f32[]{:T(128)} %constant.1.clone.1), dimensions={0}, to_apply=%region_0.0 | reduce | flops 31744 | bytes 135172 | tf_op jit(solution)/shard_map/reduce_sum | solution.py:99
  (1 shorter events, 0.0 us)
Async XLA Ops:
  0.7 10.0 %copy-start.2 = (f32[8192]{0:T(1024)S(1)}, f32[8192]{0:T(1024)}, u32[]{:S(2)}) copy-start(f32[8192]{0:T(1024)} %param.7) | copy-start | bytes 98308
  0.7 10.0 %copy-start = (s32[8192]{0:T(1024)S(1)}, s32[8192]{0:T(1024)}, u32[]{:S(2)}) copy-start(s32[8192]{0:T(1024)} %param.5) | copy-start | bytes 98308
  0.7 10.0 %copy-start.1 = (s32[8192]{0:T(1024)S(1)}, s32[8192]{0:T(1024)}, u32[]{:S(2)}) copy-start(s32[8192]{0:T(1024)} %param.6) | copy-start | bytes 98308

commit v3 on v1

v3 whole, which is shorter than its diff:
```python
import jax
import jax.numpy as jnp
from jax import lax
from jax.experimental import pallas as pl
from jax.experimental.pallas import tpu as pltpu
from jax.sharding import PartitionSpec as P

SEGMENTS = 5
QUARTERS = 28
SUBLANES = 8
LANES = 128
STEP = 8.0
SPAN = 32
PACKED = (4, LANES)
ROWS_AT_ONCE = 64
CHUNKS_AT_ONCE = 8
PARAMS = pltpu.CompilerParams(vmem_limit_bytes=4 * 2**20)


def iota(shape, dim):
    return lax.broadcasted_iota(jnp.int32, shape, dim)


def pick(lines, index):
    if len(lines) == 1:
        return lines[0]
    odd = (index & (len(lines) // 2)) != 0
    half = len(lines) // 2
    return jnp.where(odd, pick(lines[half:], index), pick(lines[:half], index))


def cube_kernel(table_ref, custkey_ref, quarter_ref, revenue_ref, out_ref, segment_ref, w1_ref, w2_ref, w3_ref):
    rows = table_ref.shape[0]
    facts = custkey_ref.shape[0]
    tile = (SUBLANES, LANES)
    zero = jnp.zeros(tile, jnp.float32)

    def look(at):
        key = custkey_ref[at, :]
        high = key >> 7
        low = key & (LANES - 1)

        def block(b, found):
            base = pl.multiple_of(b * ROWS_AT_ONCE, ROWS_AT_ONCE)
            lines = [
                jnp.take_along_axis(jnp.broadcast_to(table_ref[pl.ds(base + r, 1), :], tile), low, axis=1)
                for r in range(ROWS_AT_ONCE)
            ]
            return jnp.where((high // ROWS_AT_ONCE) == b, pick(lines, high), found)

        if rows == ROWS_AT_ONCE:
            return block(0, zero)
        return lax.fori_loop(0, rows // ROWS_AT_ONCE, block, zero)

    def add(chunk, total):
        base = pl.multiple_of(chunk * SUBLANES, SUBLANES)
        at = pl.ds(base, SUBLANES)
        found = look(at)
        segment = jnp.floor(found * (1.0 / STEP))
        weight = revenue_ref[at, :] * (found - segment * STEP)
        w1 = weight.astype(jnp.bfloat16).astype(jnp.float32)
        rest = weight - w1
        w2 = rest.astype(jnp.bfloat16).astype(jnp.float32)
        segment_ref[at, :] = segment.astype(jnp.int32)
        w1_ref[at, :] = w1
        w2_ref[at, :] = w2
        w3_ref[at, :] = rest - w2
        left, right = [], []
        for r in range(SUBLANES):
            row = pl.ds(base + r, 1)
            mine = jnp.broadcast_to(segment_ref[row, :], tile) == iota(tile, 0)
            parts = [jnp.where(mine, jnp.broadcast_to(w[row, :], tile), 0.0) for w in (w1_ref, w2_ref, w3_ref)]
            left.append(jnp.concatenate([*parts, zero], axis=0).astype(jnp.bfloat16))
            wide = (SPAN, LANES)
            hit = jnp.broadcast_to(quarter_ref[row, :], wide) == iota(wide, 0)
            right.append(jnp.where(hit, 1.0, 0.0).astype(jnp.bfloat16))
        return total + lax.dot_general(
            jnp.concatenate(left, axis=1),
            jnp.concatenate(right, axis=1),
            (((1,), (1,)), ((), ())),
            preferred_element_type=jnp.float32,
        )

    def several(step, total):
        for c in range(CHUNKS_AT_ONCE):
            total = add(step * CHUNKS_AT_ONCE + c, total)
        return total

    total = jnp.zeros((4 * SUBLANES, SPAN), jnp.float32)
    steps = facts // (SUBLANES * CHUNKS_AT_ONCE)
    total = several(0, total) if steps == 1 else lax.fori_loop(0, steps, several, total)
    cube = total[0:8] + total[8:16] + total[16:24]
    cube = jnp.concatenate([cube, jnp.zeros((SUBLANES, LANES - SPAN), jnp.float32)], axis=1)
    packed = (cube + pltpu.roll(pltpu.roll(cube, SPAN, 1), SUBLANES - PACKED[0], 0))[: PACKED[0]]
    for d in range(out_ref.shape[0]):
        out_ref[d] = packed


def sum_kernel(cubes_ref, out_ref):
    total = cubes_ref[0]
    for d in range(1, cubes_ref.shape[0]):
        total = total + cubes_ref[d]
    out_ref[: PACKED[0], :] = total[:, :QUARTERS]
    out_ref[PACKED[0] :, :] = total[: SEGMENTS - PACKED[0], SPAN : SPAN + QUARTERS]


def solution(mesh):
    shards = mesh.shape["shard"]
    everyone = shards * mesh.shape["replica"]

    def per_device(custkey, quarter, revenue, segment, rate):
        mine = segment.astype(jnp.float32) * STEP + rate.astype(jnp.float32)
        mine = mine.reshape(-1, LANES)
        table = lax.all_to_all(
            jnp.broadcast_to(mine[None], (shards, *mine.shape)), "shard", 0, 0
        )
        facts = custkey.reshape(-1, LANES).shape
        partial_cubes = pl.pallas_call(
            cube_kernel,
            out_shape=jax.ShapeDtypeStruct((everyone, *PACKED), jnp.float32),
            scratch_shapes=[pltpu.VMEM(facts, jnp.int32)] + [pltpu.VMEM(facts, jnp.float32)] * 3,
            compiler_params=PARAMS,
        )(
            table.reshape(-1, LANES),
            custkey.reshape(facts),
            quarter.reshape(facts),
            revenue.reshape(facts),
        )
        cubes = lax.all_to_all(partial_cubes, ("shard", "replica"), 0, 0)
        return pl.pallas_call(
            sum_kernel,
            out_shape=jax.ShapeDtypeStruct((SEGMENTS, QUARTERS), jnp.float32),
            compiler_params=PARAMS,
        )(cubes)

    return jax.shard_map(
        per_device,
        mesh=mesh,
        in_specs=(
            P(("shard", "replica")),
            P(("shard", "replica")),
            P(("shard", "replica")),
            P("shard"),
            P("shard"),
        ),
        out_specs=P(),
        check_vma=False,
    )
```

time: 27.8 us -> 23.9 us (0.86)
  Pallas kernels: 3.92 us -> 1.62 us
  blocking collectives: 22.3 us -> 21.2 us
  other arithmetic: 1.33 us -> 0.71 us
    pallas_call x1 -> x2, Pallas kernels: 3.92 us -> 1.62 us  [the longest x1 0.92 us: per_device(): pl.pallas_call(cube_kernel, out_shape=jax.ShapeDtypeStruct((everyone, *PA...]
    all_to_all x1, blocking collectives: 12.4 us -> 11.3 us  [per_device(): cubes = lax.all_to_all(partial_cubes, ('shard', 'replica'), 0, 0)]
    reduce_sum x1 -> x0, other arithmetic: 0.63 us -> none  [per_device(): return jnp.sum(cubes, axis=0)[:SEGMENTS, :QUARTERS]]
where the time goes in v3:
time: 23.9 us; the launch traced here: 23.6 us
  blocking collectives  21.2 us (89%)
  Pallas kernels  1.62 us (7%)
  other arithmetic  0.71 us (3%)
    all_to_all x1, blocking collectives, per_device(): cubes = lax.all_to_all(partial_cubes, ('shard', 'replica'), 0, 0)  11.3 us
    all_to_all x1, blocking collectives, per_device(): lax.all_to_all(jnp.broadcast_to(mine[None], (shards, *mine.shape)), 'shar...  9.97 us
    pallas_call x1, Pallas kernels, per_device(): pl.pallas_call(cube_kernel, out_shape=jax.ShapeDtypeStruct((everyone, *PA...  0.92 us
    broadcast_in_dim x1, other arithmetic, per_device(): jnp.broadcast_to(mine[None], (shards, *mine.shape))  0.71 us
    pallas_call x1, Pallas kernels, per_device(): pl.pallas_call(sum_kernel, out_shape=jax.ShapeDtypeStruct((SEGMENTS, QUAR...  0.69 us

profile of v3, /device:TPU:0, one launch (start us, length us, event | category | flops | bytes accessed | tf_op | source)
XLA Modules:
  0.0 23.6 jit_solution(28361698470121304)
XLA Ops:
  0.0 0.7 %add_bitcast_fusion = f32[8,128]{1,0:T(8,128)S(1)} fusion(bf16[1024]{0:T(1024)(128)(2,1)} %param.9, s32[1024]{0:T(1024)} %param.8), kind=kLoop, calls=%fused_computation | loop fusion | flops 4096 | bytes 10240 | tf_op jit(solution)/shard_map/broadcast_in_dim | solution.py:115
  0.7 0.0 copy-start.2
  0.7 0.0 copy-start
  0.7 0.0 copy-start.1
  0.7 10.0 %all_to_all.10 = f32[8,8,128]{2,1,0:T(8,128)S(1)} all-to-all(f32[8,8,128]{2,1,0:T(8,128)S(1)} %broadcast_in_dim.8), channel_id=1, replica_groups=mesh['shard'=8,'replica'=4] {'shard'}, dimensions={0} | all-to-all | bytes 65536 | tf_op jit(solution)/shard_map/all_to_all | solution.py:114
  10.7 0.0 copy-done.2
  10.7 0.0 copy-done
  10.7 0.0 copy-done.1
  10.7 0.9 %shard_map.55 = f32[32,4,128]{2,1,0:T(4,128)S(1)} custom-call(f32[64,128]{1,0:T(8,128)S(1)} %bitcast.6, s32[64,128]{1,0:T(8,128)S(1)} %bitcast.7, s32[64,128]{1,0:T(8,128)S(1)} %bitcast.8, f32[64,128]{1,0:T(8,128)S(1)} %bitcast.9), custom_call_target="tpu_custom_call" | custom-call | tf_op jit(solution)/shard_map/pallas_call | solution.py:118
  11.7 11.3 %all_to_all.11.cubes_ref = f32[32,4,128]{2,1,0:T(4,128)S(1)} all-to-all(f32[32,4,128]{2,1,0:T(4,128)S(1)} %shard_map.55), channel_id=1, replica_groups=mesh['shard'=8,'replica'=4] {'shard','replica'}, dimensions={0} | all-to-all | bytes 131072 | tf_op jit(solution)/shard_map/all_to_all | solution.py:129
  22.9 0.7 %shard_map.56 = f32[5,28]{1,0:T(8,128)} custom-call(f32[32,4,128]{2,1,0:T(4,128)S(1)} %all_to_all.11.cubes_ref), custom_call_target="tpu_custom_call" | custom-call | tf_op jit(solution)/shard_map/pallas_call | solution.py:130
  (1 shorter events, 0.0 us)
Async XLA Ops:
  0.7 10.0 %copy-start.2 = (f32[8192]{0:T(1024)S(1)}, f32[8192]{0:T(1024)}, u32[]{:S(2)}) copy-start(f32[8192]{0:T(1024)} %param.7) | copy-start | bytes 98308
  0.7 10.0 %copy-start = (s32[8192]{0:T(1024)S(1)}, s32[8192]{0:T(1024)}, u32[]{:S(2)}) copy-start(s32[8192]{0:T(1024)} %param.5) | copy-start | bytes 98308
  0.7 10.0 %copy-start.1 = (s32[8192]{0:T(1024)S(1)}, s32[8192]{0:T(1024)}, u32[]{:S(2)}) copy-start(s32[8192]{0:T(1024)} %param.6) | copy-start | bytes 98308

commit v4 on v3

--- a/solution.py
+++ b/solution.py
@@ -1,3 +1,5 @@
+import functools
+
 import jax
 import jax.numpy as jnp
 from jax import lax
@@ -10,9 +12,11 @@
 SUBLANES = 8
 LANES = 128
 STEP = 8.0
+UNIT = 512.0
+SEGMENT_BITS = 12
 SPAN = 32
 PACKED = (4, LANES)
-ROWS_AT_ONCE = 64
+WORDS_AT_ONCE = 32
 CHUNKS_AT_ONCE = 8
 PARAMS = pltpu.CompilerParams(vmem_limit_bytes=4 * 2**20)
 
@@ -29,39 +33,52 @@
     return jnp.where(odd, pick(lines[half:], index), pick(lines[:half], index))
 
 
-def cube_kernel(table_ref, custkey_ref, quarter_ref, revenue_ref, out_ref, segment_ref, w1_ref, w2_ref, w3_ref):
-    rows = table_ref.shape[0]
+def cube_kernel(order, table_ref, custkey_ref, quarter_ref, revenue_ref, out_ref, word_ref, segment_ref, w1_ref, w2_ref, w3_ref):
     facts = custkey_ref.shape[0]
+    words = word_ref.shape[0]
+    part = 2 * words // len(order)
     tile = (SUBLANES, LANES)
     zero = jnp.zeros(tile, jnp.float32)
 
+    def code(row):
+        slot = order.index(row // part)
+        return (table_ref[pl.ds(slot * part + row % part, SUBLANES), :] * UNIT).astype(jnp.int32)
+
+    for row in range(0, words, SUBLANES):
+        word_ref[pl.ds(row, SUBLANES), :] = code(row) | (code(row + words) << 16)
+
     def look(at):
         key = custkey_ref[at, :]
+        low = key & (LANES - 1)
         high = key >> 7
-        low = key & (LANES - 1)
+        second = high >= words
+        high = jnp.where(second, high - words, high)
 
         def block(b, found):
-            base = pl.multiple_of(b * ROWS_AT_ONCE, ROWS_AT_ONCE)
+            base = pl.multiple_of(b * WORDS_AT_ONCE, WORDS_AT_ONCE)
             lines = [
-                jnp.take_along_axis(jnp.broadcast_to(table_ref[pl.ds(base + r, 1), :], tile), low, axis=1)
-                for r in range(ROWS_AT_ONCE)
+                jnp.take_along_axis(jnp.broadcast_to(word_ref[pl.ds(base + r, 1), :], tile), low, axis=1)
+                for r in range(WORDS_AT_ONCE)
             ]
-            return jnp.where((high // ROWS_AT_ONCE) == b, pick(lines, high), found)
+            got = pick(lines, high)
+            return got if found is None else jnp.where(high // WORDS_AT_ONCE == b, got, found)
 
-        if rows == ROWS_AT_ONCE:
-            return block(0, zero)
-        return lax.fori_loop(0, rows // ROWS_AT_ONCE, block, zero)
+        if words == WORDS_AT_ONCE:
+            word = block(0, None)
+        else:
+            word = lax.fori_loop(0, words // WORDS_AT_ONCE, block, jnp.zeros(tile, jnp.int32))
+        return jnp.where(second, word >> 16, word & 0xFFFF)
 
     def add(chunk, total):
         base = pl.multiple_of(chunk * SUBLANES, SUBLANES)
         at = pl.ds(base, SUBLANES)
         found = look(at)
-        segment = jnp.floor(found * (1.0 / STEP))
-        weight = revenue_ref[at, :] * (found - segment * STEP)
+        rate = (found & ((1 << SEGMENT_BITS) - 1)).astype(jnp.float32) * (1.0 / UNIT)
+        weight = revenue_ref[at, :] * rate
         w1 = weight.astype(jnp.bfloat16).astype(jnp.float32)
         rest = weight - w1
         w2 = rest.astype(jnp.bfloat16).astype(jnp.float32)
-        segment_ref[at, :] = segment.astype(jnp.int32)
+        segment_ref[at, :] = found >> SEGMENT_BITS
         w1_ref[at, :] = w1
         w2_ref[at, :] = w2
         w3_ref[at, :] = rest - w2
@@ -91,9 +108,7 @@
     total = several(0, total) if steps == 1 else lax.fori_loop(0, steps, several, total)
     cube = total[0:8] + total[8:16] + total[16:24]
     cube = jnp.concatenate([cube, jnp.zeros((SUBLANES, LANES - SPAN), jnp.float32)], axis=1)
-    packed = (cube + pltpu.roll(pltpu.roll(cube, SPAN, 1), SUBLANES - PACKED[0], 0))[: PACKED[0]]
-    for d in range(out_ref.shape[0]):
-        out_ref[d] = packed
+    out_ref[...] = (cube + pltpu.roll(pltpu.roll(cube, SPAN, 1), SUBLANES - PACKED[0], 0))[: PACKED[0]]
 
 
 def sum_kernel(cubes_ref, out_ref):
@@ -105,28 +120,35 @@
 
 
 def solution(mesh):
-    shards = mesh.shape["shard"]
-    everyone = shards * mesh.shape["replica"]
+    shards, replicas = mesh.shape["shard"], mesh.shape["replica"]
+    middle = shards // 2 + 1
+    order = [middle] + [s for s in range(shards) if s != middle]
+    pairs = [(s, r) for s in range(0, shards, 2) for r in range(replicas)]
+    pairs = [pairs[-1]] + pairs[:-1]
+    halves = [[(s + (half if s + r else 1 - half)) * replicas + r for s, r in pairs] for half in (1, 0)]
 
     def per_device(custkey, quarter, revenue, segment, rate):
         mine = segment.astype(jnp.float32) * STEP + rate.astype(jnp.float32)
         mine = mine.reshape(-1, LANES)
         table = lax.all_to_all(
-            jnp.broadcast_to(mine[None], (shards, *mine.shape)), "shard", 0, 0
+            jnp.broadcast_to(mine[None], (shards, *mine.shape)), "shard", 0, 0, axis_index_groups=[order]
         )
+        table = table.reshape(-1, LANES)
         facts = custkey.reshape(-1, LANES).shape
-        partial_cubes = pl.pallas_call(
-            cube_kernel,
-            out_shape=jax.ShapeDtypeStruct((everyone, *PACKED), jnp.float32),
-            scratch_shapes=[pltpu.VMEM(facts, jnp.int32)] + [pltpu.VMEM(facts, jnp.float32)] * 3,
+        cube = pl.pallas_call(
+            functools.partial(cube_kernel, order),
+            out_shape=jax.ShapeDtypeStruct(PACKED, jnp.float32),
+            scratch_shapes=[
+                pltpu.VMEM((table.shape[0] // 2, LANES), jnp.int32),
+                pltpu.VMEM(facts, jnp.int32),
+                *[pltpu.VMEM(facts, jnp.float32)] * 3,
+            ],
             compiler_params=PARAMS,
-        )(
-            table.reshape(-1, LANES),
-            custkey.reshape(facts),
-            quarter.reshape(facts),
-            revenue.reshape(facts),
+        )(table, custkey.reshape(facts), quarter.reshape(facts), revenue.reshape(facts))
+        cube = cube + lax.ppermute(cube, "shard", [(s, s ^ 1) for s in range(shards)])
+        cubes = lax.all_to_all(
+            jnp.broadcast_to(cube[None], (len(pairs), *PACKED)), ("shard", "replica"), 0, 0, axis_index_groups=halves
         )
-        cubes = lax.all_to_all(partial_cubes, ("shard", "replica"), 0, 0)
         return pl.pallas_call(
             sum_kernel,
             out_shape=jax.ShapeDtypeStruct((SEGMENTS, QUARTERS), jnp.float32),

time: 23.9 us -> 21.2 us (0.89)
  the two profiles are of different devices: /device:TPU:0 before, /device:TPU:1 now
where the time goes in v4:
time: 21.2 us; the launch traced here: 20.9 us
  blocking collectives  17.6 us (83%)
  Pallas kernels  1.31 us (6%)
  waiting for transfers between devices  0.82 us (4%)
  other arithmetic  0.71 us (3%)
  starting transfers between devices  0.41 us (2%)
    all_to_all x1, blocking collectives, per_device(): lax.all_to_all(jnp.broadcast_to(cube[None], (len(pairs), *PACKED)), ('sha...  9.3 us
    all_to_all x1, blocking collectives, per_device(): lax.all_to_all(jnp.broadcast_to(mine[None], (shards, *mine.shape)), 'shar...  8.33 us
    ppermute x1, waiting for transfers between devices, per_device(): lax.ppermute(cube, 'shard', [(s, s ^ 1) for s in range(shards)])  0.82 us
    broadcast_in_dim x1, other arithmetic, per_device(): jnp.broadcast_to(mine[None], (shards, *mine.shape))  0.71 us
    pallas_call x1, Pallas kernels, per_device(): pl.pallas_call(sum_kernel, out_shape=jax.ShapeDtypeStruct((SEGMENTS, QUAR...  0.68 us
    pallas_call x1, Pallas kernels, per_device(): pl.pallas_call(functools.partial(cube_kernel, order), out_shape=jax.Shape...  0.63 us
  transfers between devices with their start and end apart: 1, of which 1 were waited for; matrix products, arithmetic and copies ran while one was open for 0% of the time, Pallas kernels for 0%

profile of v4, /device:TPU:1, one launch (start us, length us, event | category | flops | bytes accessed | tf_op | source)
XLA Modules:
  0.0 20.9 jit_solution(12669836117989346836)
XLA Ops:
  0.0 0.7 %add_bitcast_fusion = f32[8,128]{1,0:T(8,128)S(1)} fusion(bf16[1024]{0:T(1024)(128)(2,1)} %param.9, s32[1024]{0:T(1024)} %param.8), kind=kLoop, calls=%fused_computation | loop fusion | flops 4096 | bytes 10240 | tf_op jit(solution)/shard_map/broadcast_in_dim | solution.py:134
  0.7 0.0 copy-start.2
  0.7 0.0 copy-start
  0.7 0.0 copy-start.1
  0.7 8.3 %all_to_all.10 = f32[8,8,128]{2,1,0:T(8,128)S(1)} all-to-all(f32[8,8,128]{2,1,0:T(8,128)S(1)} %broadcast_in_dim.14), channel_id=1, replica_groups={{20,0,4,8,12,16,24,28},{21,1,5,9,13,17,25,29},{22,2,6,10,14,18,26,30},{..., dimensions={0} | all-to-all | bytes 65536 | tf_op jit(solution)/shard_map/all_to_all | solution.py:133
  9.1 0.0 copy-done.2
  9.1 0.0 copy-done
  9.1 0.0 copy-done.1
  9.1 0.6 %shard_map.55 = f32[4,128]{1,0:T(4,128)S(1)} custom-call(f32[64,128]{1,0:T(8,128)S(1)} %bitcast.6, s32[64,128]{1,0:T(8,128)S(1)} %bitcast.7, s32[64,128]{1,0:T(8,128)S(1)} %bitcast.8, f32[64,128]{1,0:T(8,128)S(1)} %bitcast.9), custom_call_target="tpu_custom_call" | custom-call | tf_op jit(solution)/shard_map/pallas_call | solution.py:138
  9.7 0.4 %collective-permute-start = (f32[4,128]{1,0:T(4,128)S(1)}, f32[4,128]{1,0:T(4,128)S(1)}, u32[]{:S(2)}, u32[]{:S(2)}) collective-permute-start(f32[4,128]{1,0:T(4,128)S(1)} %shard_map.55), channel_id=1, source_target_pairs={{0,4},{4,0},{8,12},{12,8},{16,20},{20,16},{24,28},{28,24},{1,5},{5... | collective-permute-start | bytes 6152 | tf_op jit(solution)/shard_map/ppermute | solution.py:148
  10.1 0.8 %collective-permute-done = f32[4,128]{1,0:T(4,128)S(1)} collective-permute-done((f32[4,128]{1,0:T(4,128)S(1)}, f32[4,128]{1,0:T(4,128)S(1)}, u32[]{:S(2)}, u32[]{:S(2)}) %collective-permute-start) | collective-permute-done | bytes 2080 | tf_op jit(solution)/shard_map/ppermute | solution.py:148
  11.0 9.3 %all_to_all.11.cubes_ref = f32[16,4,128]{2,1,0:T(4,128)S(1)} all-to-all(f32[16,4,128]{2,1,0:T(4,128)S(1)} %broadcast_in_dim.15), channel_id=1, replica_groups={{31,0,5,6,7,12,13,14,15,20,21,22,23,28,29,30},{27,4,1,2,3,8,9,10,11,16,..., dimensions={0} | all-to-all | bytes 65536 | tf_op jit(solution)/shard_map/all_to_all | solution.py:149
  20.3 0.7 %shard_map.56 = f32[5,28]{1,0:T(8,128)} custom-call(f32[16,4,128]{2,1,0:T(4,128)S(1)} %all_to_all.11.cubes_ref), custom_call_target="tpu_custom_call" | custom-call | tf_op jit(solution)/shard_map/pallas_call | solution.py:152
  (3 shorter events, 0.0 us)
Async XLA Ops:
  0.7 8.4 %copy-start.2 = (f32[8192]{0:T(1024)S(1)}, f32[8192]{0:T(1024)}, u32[]{:S(2)}) copy-start(f32[8192]{0:T(1024)} %param.7) | copy-start | bytes 98308
  0.7 8.4 %copy-start = (s32[8192]{0:T(1024)S(1)}, s32[8192]{0:T(1024)}, u32[]{:S(2)}) copy-start(s32[8192]{0:T(1024)} %param.5) | copy-start | bytes 98308
  0.7 8.3 %copy-start.1 = (s32[8192]{0:T(1024)S(1)}, s32[8192]{0:T(1024)}, u32[]{:S(2)}) copy-start(s32[8192]{0:T(1024)} %param.6) | copy-start | bytes 98308
  9.7 1.2 %collective-permute-start = (f32[4,128]{1,0:T(4,128)S(1)}, f32[4,128]{1,0:T(4,128)S(1)}, u32[]{:S(2)}, u32[]{:S(2)}) collective-permute-start(f32[4,128]{1,0:T(4,128)S(1)} %shard_map.55), channel_id=1, source_target_pairs={{0,4},{4,0},{8,12},{12,8},{16,20},{20,16},{24,28},{28,24},{1,5},{5... | collective-permute-start | bytes 6152 | tf_op jit(solution)/shard_map/ppermute | solution.py:148
